TPU v7x, 32 devices: a whole 2x2x4 slice. The times are simulated.
32 devices in a mesh: expert: 16 (over z, y, core), dp: 2 (over x).
Axes of the slice: x: 2, y: 2, z: 4, core: 2. Of those that a mesh axis runs over, the one named last changes fastest.
Arguments:
- tokens: bfloat16 [4096, 7168], P(('expert', 'dp')), may hold values from -6 to 6
- cotangent: bfloat16 [4096, 7168], P(('expert', 'dp')), may hold values from -1.5 to 1.5
- routes: int32 [4096, 8], P(('expert', 'dp')), may hold values from 0 to 255, all different within a row; in each aligned block of 128 rows (0 to 127, 128 to 255, ...) at most 9 rows name the same one
- route_gates: float32 [4096, 8], P(('expert', 'dp')), may hold values from 0.1 to 1
- gate_weight: bfloat16 [16, 7168, 256], P('expert'), may hold values from -0.0625 to 0.0625
- up_weight: bfloat16 [16, 7168, 256], P('expert'), may hold values from -0.0625 to 0.0625
- down_weight: bfloat16 [16, 256, 7168], P('expert'), may hold values from -0.125 to 0.125
Outputs:
- grad_gate: bfloat16 [16, 7168, 256], P('expert')
- grad_up: bfloat16 [16, 7168, 256], P('expert')
- grad_down: bfloat16 [16, 256, 7168], P('expert')
Inputs may be any that keep to these rules, and one draw needn't show every extreme that they name: `routes`: each row names 8 different experts; among the rows of one device no expert is named more than 9 times.
All inputs are finite; a program needn't handle non-finite values.
Results may differ from a plain program's by a relative error of at most 0.0065.
Values may be sent and summed in bfloat16 or wider, within the bound.
No kernel may reach another device: no remote copies, remote signals or barrier semaphores. Data moves between devices by JAX's collectives and lax.ppermute only.
A program may use at most 192 MiB of HBM per device.

v0:
```python
import jax
import jax.numpy as jnp
from jax import lax
from jax.sharding import PartitionSpec as P

HIDDEN_SIZE = 2048
SLICE_UNITS = 256
CAP = 9


def swapped(block, axis, bit):
    count = lax.axis_size(axis)
    route = []
    for low in range(count):
        high = low | 1 << bit
        if high != low and high < count:
            route += [(low, high), (high, low)]
    return lax.ppermute(block, axis, route)


def slice_grads(inputs, scaled, gate_parts, up_parts, down_parts, form):
    gate_pre = jnp.einsum(form + ",pwh->rh", inputs, gate_parts, preferred_element_type=jnp.float32)
    up_pre = jnp.einsum(form + ",pwh->rh", inputs, up_parts, preferred_element_type=jnp.float32)
    sigmoid = jax.nn.sigmoid(gate_pre)
    active = gate_pre * sigmoid
    hidden = (active * up_pre).astype(jnp.bfloat16)
    back_hidden = jnp.einsum(
        form + ",hpw->rh", scaled, down_parts, preferred_element_type=jnp.float32
    )
    gate_delta = (back_hidden * up_pre * sigmoid * (1.0 + gate_pre * (1.0 - sigmoid))).astype(
        jnp.bfloat16
    )
    up_delta = (back_hidden * active).astype(jnp.bfloat16)
    gate_term = jnp.einsum(
        form + ",rh->pwh", inputs, gate_delta, preferred_element_type=jnp.float32
    )
    up_term = jnp.einsum(form + ",rh->pwh", inputs, up_delta, preferred_element_type=jnp.float32)
    down_term = jnp.einsum(
        "rh," + form + "->hpw", hidden, scaled, preferred_element_type=jnp.float32
    )
    return (gate_term, up_term, down_term)


def on_device(tokens, cotangent, routes, route_gates, gate_weight, up_weight, down_weight):
    slices = HIDDEN_SIZE // SLICE_UNITS
    experts_all = lax.axis_size("expert")
    window = experts_all // slices
    capacity = CAP
    model_width = tokens.shape[1]
    part_width = model_width // slices
    units = gate_weight.shape[2]
    top_count = routes.shape[1]
    flat_routes = routes.reshape(-1)
    flat_gates = route_gates.reshape(-1)
    inside = flat_routes < window
    member = ((flat_routes[:, None] == jnp.arange(window)[None, :]) & inside[:, None]).astype(
        jnp.int32
    )
    earlier = jnp.cumsum(member, axis=0) - member
    slot_index = jnp.sum(earlier * member, axis=1)
    target = jnp.where(inside, flat_routes * capacity + slot_index, -1)
    landing = target[:, None] == jnp.arange(window * capacity)[None, :]
    owning = jnp.arange(flat_routes.shape[0]) // top_count
    source = jnp.sum(jnp.where(landing, owning[:, None], 0), axis=0)
    weight = jnp.sum(jnp.where(landing, flat_gates[:, None], 0.0), axis=0)
    sent_inputs = tokens[source].reshape(window, capacity, model_width)
    sent_scaled = (weight[:, None] * cotangent[source].astype(jnp.float32)).astype(jnp.bfloat16)
    sent_scaled = sent_scaled.reshape(window, capacity, model_width)
    gate_parts = gate_weight[0].reshape(slices, part_width, units)
    up_parts = up_weight[0].reshape(slices, part_width, units)
    down_parts = down_weight[0].reshape(units, slices, part_width)

    def columns_out(block):
        shaped = block.reshape(window, capacity, slices, part_width)
        return jnp.transpose(shaped, (0, 2, 1, 3)).reshape(window * slices, capacity, part_width)

    held_inputs, held_scaled = (
        lax.all_to_all(columns_out(sent_inputs), "expert", split_axis=0, concat_axis=0, tiled=True),
        lax.all_to_all(columns_out(sent_scaled), "expert", split_axis=0, concat_axis=0, tiled=True),
    )
    held_inputs = held_inputs.reshape(1, -1, part_width)
    held_scaled = held_scaled.reshape(1, -1, part_width)
    for level in range(3):
        other_inputs, other_scaled = swapped((held_inputs, held_scaled), "expert", level)
        held_inputs = jnp.concatenate((held_inputs, other_inputs), axis=0)
        held_scaled = jnp.concatenate((held_scaled, other_scaled), axis=0)
    local = jnp.bitwise_and(lax.axis_index("expert"), slices - 1)
    order = jnp.bitwise_xor(local, jnp.arange(slices, dtype=jnp.int32))
    gate_term, up_term, down_term = slice_grads(
        held_inputs,
        held_scaled,
        jnp.take(gate_parts, order, axis=0),
        jnp.take(up_parts, order, axis=0),
        jnp.take(down_parts, order, axis=1),
        "prw",
    )
    gate_term = jnp.take(gate_term, order, axis=0)
    up_term = jnp.take(up_term, order, axis=0)
    down_term = jnp.take(down_term, order, axis=1)
    gate_term = gate_term.reshape(model_width, units)
    up_term = up_term.reshape(model_width, units)
    down_term = down_term.reshape(units, model_width)
    gate_sum, up_sum, down_sum = (
        lax.psum(gate_term.astype(jnp.bfloat16), "dp").astype(jnp.float32),
        lax.psum(up_term.astype(jnp.bfloat16), "dp").astype(jnp.float32),
        lax.psum(down_term.astype(jnp.bfloat16), "dp").astype(jnp.float32),
    )
    grad_gate = gate_sum.astype(jnp.bfloat16)
    grad_up = up_sum.astype(jnp.bfloat16)
    grad_down = down_sum.astype(jnp.bfloat16)
    return (grad_gate[None], grad_up[None], grad_down[None])


def solution(mesh):
    return jax.shard_map(
        on_device,
        mesh=mesh,
        in_specs=(
            P(("expert", "dp"), None),
            P(("expert", "dp"), None),
            P(("expert", "dp"), None),
            P(("expert", "dp"), None),
            P("expert", None, None),
            P("expert", None, None),
            P("expert", None, None),
        ),
        out_specs=(P("expert", None, None), P("expert", None, None), P("expert", None, None)),
        check_vma=False,
    )
```

profile of v0, /device:TPU:0, one launch (start us, length us, event | category | flops | bytes accessed | tf_op | source)
XLA Modules:
  0.0 427.9 jit_solution(543016347699956142)
XLA Ops:
  11.2 7.4 %all-to-all-start = ((bf16[16,9,896]{2,1,0:T(8,128)(2,1)}), bf16[16,9,896]{2,1,0:T(8,128)(2,1)S(1)}, u32[]{:S(2)}, u32[]{:S(2)}) async-start(bf16[16,9,896]{2,1,0:T(8,128)(2,1)} %bitcast.4), calls=%async_computation | async-start | bytes 917504 | tf_op jit(solution)/shard_map/all_to_all | solution.py:78
  20.0 11.8 %all-to-all-done = bf16[16,9,896]{2,1,0:T(8,128)(2,1)S(1)} async-done(((bf16[16,9,896]{2,1,0:T(8,128)(2,1)}), bf16[16,9,896]{2,1,0:T(8,128)(2,1)S(1)}, u32[]{:S(2)}, u32[]{:S(2)}) %all-to-all-start) | async-done | bytes 258080 | tf_op jit(solution)/shard_map/all_to_all | solution.py:78
  33.1 4.1 all-to-all-start.1
  37.3 2.0 collective-permute-start.1
  39.3 11.1 %all-to-all-done.1 = bf16[16,9,896]{2,1,0:T(8,128)(2,1)S(1)} async-done(((bf16[16,9,896]{2,1,0:T(8,128)(2,1)}), bf16[16,9,896]{2,1,0:T(8,128)(2,1)S(1)}, u32[]{:S(2)}, u32[]{:S(2)}) %all-to-all-start.1) | async-done | bytes 258080 | tf_op jit(solution)/shard_map/all_to_all | solution.py:79
  50.7 5.5 %collective-permute-done.1 = bf16[2,144,896]{2,1,0:T(8,128)(2,1)S(1)} collective-permute-done((bf16[2,144,896]{2,1,0:T(8,128)(2,1)S(1)}, bf16[2,144,896]{2,1,0:T(8,128)(2,1)S(1)}, u32[]{:S(2)}, u32[]{:S(2)}) %collective-permute-start.1) | collective-permute-done | bytes 516128 | tf_op jit(solution)/shard_map/ppermute | solution.py:18
  60.4 4.7 %gather_fusion.5 = bf16[8,896,256]{2,1,0:T(8,128)(2,1)} fusion(bf16[8,896,256]{2,1,0:T(8,128)(2,1)} %bitcast.81, s32[1024]{0:T(1024)S(1)} %pad_clamp_fusion), kind=kCustom, calls=%fused_computation.2.clone | custom fusion | bytes 7340064 | tf_op jit(solution)/shard_map/jit(_take)/gather | solution.py:92
  65.0 4.6 %gather_fusion.4 = bf16[8,896,256]{2,1,0:T(8,128)(2,1)} fusion(bf16[8,896,256]{2,1,0:T(8,128)(2,1)} %bitcast.82, s32[1024]{0:T(1024)S(1)} %pad_clamp_fusion), kind=kCustom, calls=%fused_computation.clone | custom fusion | bytes 7340064 | tf_op jit(solution)/shard_map/jit(_take)/gather | solution.py:93
  69.6 5.9 %copy.33 = bf16[1,256,7168]{1,2,0:T(8,128)(2,1)} copy(bf16[1,256,7168]{2,1,0:T(8,128)(2,1)} %param.17) | data formatting | bytes 7340032 | tf_op args[6]
  75.5 6.2 %copy.34 = bf16[256,8,896]{2,0,1:T(8,128)(2,1)} copy(bf16[256,8,896]{0,2,1:T(8,128)(2,1)} %bitcast.76) | data formatting | bytes 7340032 | tf_op jit(solution)/shard_map/reshape;squeeze | solution.py:71
  81.7 4.8 %gather_fusion.2 = bf16[8,256,896]{2,1,0:T(8,128)(2,1)} fusion(bf16[256,8,896]{2,0,1:T(8,128)(2,1)} %copy.34, s32[1024]{0:T(1024)S(1)} %pad_clamp_fusion.1), kind=kCustom, calls=%fused_computation.6 | custom fusion | bytes 7340064 | tf_op jit(solution)/shard_map/jit(_take)/gather | solution.py:94
  91.5 19.3 %collective-permute-done.5 = bf16[4,144,896]{2,1,0:T(8,128)(2,1)S(1)} collective-permute-done((bf16[4,144,896]{2,1,0:T(8,128)(2,1)S(1)}, bf16[4,144,896]{2,1,0:T(8,128)(2,1)S(1)}, u32[]{:S(2)}, u32[]{:S(2)}) %collective-permute-start.5) | collective-permute-done | bytes 1032224 | tf_op jit(solution)/shard_map/ppermute | solution.py:18
  112.4 3.0 fusion.29
  115.4 3.1 fusion.31
  118.5 3.1 fusion.26
  121.5 4.8 %gather_fusion.3 = bf16[8,256,896]{2,1,0:T(8,128)(2,1)} fusion(bf16[256,8,896]{2,0,1:T(8,128)(2,1)} %fusion.29, s32[1024]{0:T(1024)S(1)} %pad_clamp_fusion.1), kind=kCustom, calls=%fused_computation.7 | custom fusion | bytes 7340064 | tf_op jit(solution)/shard_map/jit(_take)/gather | solution.py:99
  126.3 6.3 %copy.35 = bf16[256,8,896]{0,2,1:T(8,128)(2,1)} copy(bf16[256,8,896]{2,0,1:T(8,128)(2,1)} %bitcast.77) | data formatting | bytes 7340032 | tf_op jit(solution)/shard_map/jit(_take)/gather | solution.py:99
  132.6 4.7 %gather_fusion.6 = bf16[8,896,256]{2,1,0:T(8,128)(2,1)} fusion(bf16[8,896,256]{2,1,0:T(8,128)(2,1)} %fusion.31, s32[1024]{0:T(1024)S(1)} %pad_clamp_fusion), kind=kCustom, calls=%fused_computation.1.clone | custom fusion | bytes 7340064 | tf_op jit(solution)/shard_map/jit(_take)/gather | solution.py:97
  137.3 4.7 %gather_fusion.7 = bf16[8,896,256]{2,1,0:T(8,128)(2,1)} fusion(bf16[8,896,256]{2,1,0:T(8,128)(2,1)} %fusion.26, s32[1024]{0:T(1024)S(1)} %pad_clamp_fusion), kind=kCustom, calls=%fused_computation.3.clone | custom fusion | bytes 7340064 | tf_op jit(solution)/shard_map/jit(_take)/gather | solution.py:98
  141.9 7.3 %fusion = bf16[256,7168]{0,1:T(8,128)(2,1)} fusion(bf16[256,8,896]{0,2,1:T(8,128)(2,1)} %copy.35, pred[7168]{0:T(1024)(128)(4,1)S(1)} %broadcast_in_dim.100), kind=kLoop, calls=%fused_computation.9 | loop fusion | flops 1835008 | bytes 7347200 | tf_op jit(solution)/shard_map/convert_element_type | solution.py:106
  149.2 5.1 %select_convert_fusion = (bf16[8,896,256]{2,1,0:T(8,128)(2,1)}, bf16[8,896,256]{2,1,0:T(8,128)(2,1)}) fusion(bf16[8,896,256]{2,1,0:T(8,128)(2,1)S(1)} %copy-done.3, pred[8]{0:T(512)(128)(4,1)S(1)} %compare_and_fusion.1, bf16[8,896,256]{2,1,0:T(8,128)(2,1)S(1)} %copy-done.2), kind=kLoop, calls=%fused_computation.10 | loop fusion | flops 3670016 | bytes 14680072 | tf_op jit(solution)/shard_map/convert_element_type | solution.py:105
  154.3 254.7 %all-reduce.3.cloned.1.call-done = (bf16[1,7168,256]{2,1,0:T(8,128)(2,1)}, bf16[1,7168,256]{2,1,0:T(8,128)(2,1)}, bf16[1,256,7168]{1,2,0:T(8,128)(2,1)}) async-done(((bf16[1,7168,256]{2,1,0:T(8,128)(2,1)}, bf16[1,7168,256]{2,1,0:T(8,128)(2,1)}, bf16[1,256,7168]{1,2,0:T(8,128)(2,1)}), (bf16[1,7168,256]{2,1,0:T(8,128)(2,1)}, bf16[1,7168,256]{2,1,0:T(8,128)(2,1)}, ...) | async-done | bytes 11010064 | tf_op jit(solution)/shard_map/psum | solution.py:104
  409.0 5.9 %copy.36 = bf16[1,256,7168]{2,1,0:T(8,128)(2,1)} copy(bf16[1,256,7168]{1,2,0:T(8,128)(2,1)} %get-tuple-element.16) | data formatting | bytes 7340032
  414.9 4.3 copy.50
  (85 shorter events, 19.4 us)
Async XLA Ops:
  7.2 2.4 copy-start
  7.2 11.5 %copy-start.9 = (f32[128,8]{0,1:T(8,128)S(1)}, f32[128,8]{0,1:T(8,128)}, u32[]{:S(2)}) copy-start(f32[128,8]{0,1:T(8,128)} %param.14) | copy-start | bytes 12292
  10.3 8.7 %copy-start.4 = (bf16[128,7168]{1,0:T(8,128)(2,1)S(1)}, bf16[128,7168]{1,0:T(8,128)(2,1)}, u32[]{:S(2)}) copy-start(bf16[128,7168]{1,0:T(8,128)(2,1)} %param.12) | copy-start | bytes 5505028
  11.2 20.6 %all-to-all-start = ((bf16[16,9,896]{2,1,0:T(8,128)(2,1)}), bf16[16,9,896]{2,1,0:T(8,128)(2,1)S(1)}, u32[]{:S(2)}, u32[]{:S(2)}) async-start(bf16[16,9,896]{2,1,0:T(8,128)(2,1)} %bitcast.4), calls=%async_computation | async-start | bytes 917504 | tf_op jit(solution)/shard_map/all_to_all | solution.py:78
  32.0 5.2 %collective-permute-start = (bf16[1,144,896]{2,1,0:T(8,128)(2,1)S(1)}, bf16[1,144,896]{2,1,0:T(8,128)(2,1)S(1)}, u32[]{:S(2)}, u32[]{:S(2)}) collective-permute-start(bf16[1,144,896]{2,1,0:T(8,128)(2,1)S(1)} %reshape.137), channel_id=1, source_target_pairs={{0,2},{2,0},{4,6},{6,4},{8,10},{10,8},{12,14},{14,12},{16,18},{18,... | collective-permute-start | bytes 774152 | tf_op jit(solution)/shard_map/ppermute | solution.py:18
  33.1 17.3 %all-to-all-start.1 = ((bf16[16,9,896]{2,1,0:T(8,128)(2,1)}), bf16[16,9,896]{2,1,0:T(8,128)(2,1)S(1)}, u32[]{:S(2)}, u32[]{:S(2)}) async-start(bf16[16,9,896]{2,1,0:T(8,128)(2,1)} %bitcast.6), calls=%async_computation.1 | async-start | bytes 917504 | tf_op jit(solution)/shard_map/all_to_all | solution.py:79
  37.2 371.8 %all-reduce.3.cloned.1.call-start = ((), (), s32[]{:S(2)}) async-start(), calls=%async_computation.2 | async-start | bytes 22020096 | tf_op jit(solution)/shard_map/psum | solution.py:104
  37.3 18.9 %collective-permute-start.1 = (bf16[2,144,896]{2,1,0:T(8,128)(2,1)S(1)}, bf16[2,144,896]{2,1,0:T(8,128)(2,1)S(1)}, u32[]{:S(2)}, u32[]{:S(2)}) collective-permute-start(bf16[2,144,896]{2,1,0:T(8,128)(2,1)S(1)} %pad_maximum_fusion.2), channel_id=1, source_target_pairs={{0,4},{4,0},{2,6},{6,2},{8,12},{12,8},{10,14},{14,10},{16,20},{20,... | collective-permute-start | bytes 1548296 | tf_op jit(solution)/shard_map/ppermute | solution.py:18
  50.5 8.3 %collective-permute-start.3 = (bf16[1,144,896]{2,1,0:T(8,128)(2,1)S(1)}, bf16[1,144,896]{2,1,0:T(8,128)(2,1)S(1)}, u32[]{:S(2)}, u32[]{:S(2)}) collective-permute-start(bf16[1,144,896]{2,1,0:T(8,128)(2,1)S(1)} %reshape.139), channel_id=1, source_target_pairs={{0,2},{2,0},{4,6},{6,4},{8,10},{10,8},{12,14},{14,12},{16,18},{18,... | collective-permute-start | bytes 774152 | tf_op jit(solution)/shard_map/ppermute | solution.py:18
  57.4 30.2 %collective-permute-start.2 = (bf16[4,144,896]{2,1,0:T(8,128)(2,1)}, bf16[4,144,896]{2,1,0:T(8,128)(2,1)S(1)}, u32[]{:S(2)}, u32[]{:S(2)}) collective-permute-start(bf16[4,144,896]{2,1,0:T(8,128)(2,1)} %pad_maximum_fusion), channel_id=1, source_target_pairs={{0,8},{8,0},{2,10},{10,2},{4,12},{12,4},{6,14},{14,6},{16,24},{24,... | collective-permute-start | bytes 3096584 | tf_op jit(solution)/shard_map/ppermute | solution.py:18
  59.7 27.0 %collective-permute-start.4 = (bf16[2,144,896]{2,1,0:T(8,128)(2,1)}, bf16[2,144,896]{2,1,0:T(8,128)(2,1)S(1)}, u32[]{:S(2)}, u32[]{:S(2)}) collective-permute-start(bf16[2,144,896]{2,1,0:T(8,128)(2,1)} %pad_maximum_fusion.3), channel_id=1, source_target_pairs={{0,4},{4,0},{2,6},{6,2},{8,12},{12,8},{10,14},{14,10},{16,20},{20,... | collective-permute-start | bytes 1548296 | tf_op jit(solution)/shard_map/ppermute | solution.py:18
  86.6 2.0 copy-start.8
  86.9 23.9 %collective-permute-start.5 = (bf16[4,144,896]{2,1,0:T(8,128)(2,1)S(1)}, bf16[4,144,896]{2,1,0:T(8,128)(2,1)S(1)}, u32[]{:S(2)}, u32[]{:S(2)}) collective-permute-start(bf16[4,144,896]{2,1,0:T(8,128)(2,1)S(1)} %pad_maximum_fusion.1), channel_id=1, source_target_pairs={{0,8},{8,0},{2,10},{10,2},{4,12},{12,4},{6,14},{14,6},{16,24},{24,... | collective-permute-start | bytes 3096584 | tf_op jit(solution)/shard_map/ppermute | solution.py:18
  88.7 2.0 copy-start.7
  90.7 20.2 %copy-start.6 = (bf16[8,256,896]{2,1,0:T(8,128)(2,1)S(1)}, bf16[8,256,896]{2,1,0:T(8,128)(2,1)}, u32[]{:S(2)}) copy-start(bf16[8,256,896]{2,1,0:T(8,128)(2,1)} %gather_fusion.2) | copy-start | bytes 11010052
  141.9 7.3 %copy-start.2 = (bf16[8,896,256]{2,1,0:T(8,128)(2,1)S(1)}, bf16[8,896,256]{2,1,0:T(8,128)(2,1)}, u32[]{:S(2)}) copy-start(bf16[8,896,256]{2,1,0:T(8,128)(2,1)} %gather_fusion.6) | copy-start | bytes 11010052
  141.9 7.3 %copy-start.3 = (bf16[8,896,256]{2,1,0:T(8,128)(2,1)S(1)}, bf16[8,896,256]{2,1,0:T(8,128)(2,1)}, u32[]{:S(2)}) copy-start(bf16[8,896,256]{2,1,0:T(8,128)(2,1)} %gather_fusion.7) | copy-start | bytes 11010052
  414.9 4.3 copy-start.5
  414.9 6.1 %copy-start.1 = (bf16[128,7168]{1,0:T(8,128)(2,1)S(1)}, bf16[128,7168]{1,0:T(8,128)(2,1)}, u32[]{:S(2)}) copy-start(bf16[128,7168]{1,0:T(8,128)(2,1)} %param.11) | copy-start | bytes 5505028
Sparse Core Ops, SparseCore 0:
  154.4 254.5 all-reduce.2
where the time goes:
time: 429 us; the launch traced here: 428 us
  waiting for transfers between devices  302 us (70%)
  local copies, waits for them, and re-layouts  66.6 us (16%)
  starting transfers between devices  16.5 us (4%)
  other arithmetic  15.8 us (4%)
  between operations  14.3 us (3%)
  matrix products  12.2 us (3%)
    psum x1, waiting for transfers between devices, on_device(): lax.psum(gate_term.astype(jnp.bfloat16), 'dp').astype(jnp.float32)  255 us
    ppermute x6, waiting for transfers between devices, swapped(): return lax.ppermute(block, axis, route)  24.8 us
    unnamed x36, local copies, waits for them, and re-layouts  21.6 us
    all_to_all x1, waiting for transfers between devices, on_device(): lax.all_to_all(columns_out(sent_inputs), 'expert', split_axis=0, concat_a...  11.8 us
    all_to_all x1, waiting for transfers between devices, on_device(): lax.all_to_all(columns_out(sent_scaled), 'expert', split_axis=0, concat_a...  11.1 us
    gather x2, local copies, waits for them, and re-layouts, on_device(): down_term = jnp.take(down_term, order, axis=1)  11.1 us
  transfers between devices with their start and end apart: 9, of which 5 were waited for; matrix products, arithmetic and copies ran while one was open for 8% of the time, Pallas kernels for 0%

commit v1 on v0

--- a/solution.py
+++ b/solution.py
@@ -6,6 +6,11 @@
 HIDDEN_SIZE = 2048
 SLICE_UNITS = 256
 CAP = 9
+
+
+def ports_obtain(s0):
+    opened = lax.all_gather(s0, axis_name="dp").sum(axis=0)
+    return opened
 
 
 def swapped(block, axis, bit):
@@ -101,7 +106,7 @@
     up_term = up_term.reshape(model_width, units)
     down_term = down_term.reshape(units, model_width)
     gate_sum, up_sum, down_sum = (
-        lax.psum(gate_term.astype(jnp.bfloat16), "dp").astype(jnp.float32),
+        ports_obtain(gate_term.astype(jnp.bfloat16)).astype(jnp.float32),
         lax.psum(up_term.astype(jnp.bfloat16), "dp").astype(jnp.float32),
         lax.psum(down_term.astype(jnp.bfloat16), "dp").astype(jnp.float32),
     )

time: 429 us -> 444 us (1.035)
  waiting for transfers between devices: 302 us -> 312 us
  other arithmetic: 15.8 us -> 23 us
    all_gather x0 -> x1, waiting for transfers between devices: none -> 88.4 us  [ports_obtain(): opened = lax.all_gather(s0, axis_name='dp').sum(axis=0)]
    psum x1, waiting for transfers between devices: 255 us -> 175 us  [on_device(): lax.psum(up_term.astype(jnp.bfloat16), 'dp').astype(jnp.float32)]
    reduce_sum x0 -> x1, other arithmetic: none -> 7.14 us  [ports_obtain(): opened = lax.all_gather(s0, axis_name='dp').sum(axis=0)]
    unnamed x36 -> x33, local copies, waits for them, and re-layouts: 21.6 us -> 19.7 us
  transfers between devices with their start and end apart: 9 -> 10, of which waited for: 5 -> 6; matrix products, arithmetic and copies ran while one was open for 8% -> 9% of each run, Pallas kernels for 0% -> 0%
where the time goes in v1:
time: 444 us; the launch traced here: 443 us
  waiting for transfers between devices  312 us (70%)
  local copies, waits for them, and re-layouts  64.8 us (15%)
  other arithmetic  23 us (5%)
  starting transfers between devices  16.5 us (4%)
  between operations  14.4 us (3%)
  matrix products  12.2 us (3%)
    psum x1, waiting for transfers between devices, on_device(): lax.psum(up_term.astype(jnp.bfloat16), 'dp').astype(jnp.float32)  175 us
    all_gather x1, waiting for transfers between devices, ports_obtain(): opened = lax.all_gather(s0, axis_name='dp').sum(axis=0)  88.4 us
    ppermute x6, waiting for transfers between devices, swapped(): return lax.ppermute(block, axis, route)  24.8 us
    unnamed x33, local copies, waits for them, and re-layouts  19.7 us
    all_to_all x1, waiting for transfers between devices, on_device(): lax.all_to_all(columns_out(sent_inputs), 'expert', split_axis=0, concat_a...  11.8 us
    gather x2, local copies, waits for them, and re-layouts, on_device(): down_term = jnp.take(down_term, order, axis=1)  11.1 us
    all_to_all x1, waiting for transfers between devices, on_device(): lax.all_to_all(columns_out(sent_scaled), 'expert', split_axis=0, concat_a...  11.1 us
  transfers between devices with their start and end apart: 10, of which 6 were waited for; matrix products, arithmetic and copies ran while one was open for 9% of the time, Pallas kernels for 0%

profile of v1, /device:TPU:0, one launch (start us, length us, event | category | flops | bytes accessed | tf_op | source)
XLA Modules:
  0.0 442.9 jit_solution(5999851007914981024)
XLA Ops:
  11.2 7.4 %all-to-all-start = ((bf16[16,9,896]{2,1,0:T(8,128)(2,1)}), bf16[16,9,896]{2,1,0:T(8,128)(2,1)S(1)}, u32[]{:S(2)}, u32[]{:S(2)}) async-start(bf16[16,9,896]{2,1,0:T(8,128)(2,1)} %bitcast.4), calls=%async_computation | async-start | bytes 917504 | tf_op jit(solution)/shard_map/all_to_all | solution.py:83
  20.0 11.8 %all-to-all-done = bf16[16,9,896]{2,1,0:T(8,128)(2,1)S(1)} async-done(((bf16[16,9,896]{2,1,0:T(8,128)(2,1)}), bf16[16,9,896]{2,1,0:T(8,128)(2,1)S(1)}, u32[]{:S(2)}, u32[]{:S(2)}) %all-to-all-start) | async-done | bytes 258080 | tf_op jit(solution)/shard_map/all_to_all | solution.py:83
  33.1 4.1 all-to-all-start.1
  39.3 11.1 %all-to-all-done.1 = bf16[16,9,896]{2,1,0:T(8,128)(2,1)S(1)} async-done(((bf16[16,9,896]{2,1,0:T(8,128)(2,1)}), bf16[16,9,896]{2,1,0:T(8,128)(2,1)S(1)}, u32[]{:S(2)}, u32[]{:S(2)}) %all-to-all-start.1) | async-done | bytes 258080 | tf_op jit(solution)/shard_map/all_to_all | solution.py:84
  50.7 5.5 %collective-permute-done.1 = bf16[2,144,896]{2,1,0:T(8,128)(2,1)S(1)} collective-permute-done((bf16[2,144,896]{2,1,0:T(8,128)(2,1)S(1)}, bf16[2,144,896]{2,1,0:T(8,128)(2,1)S(1)}, u32[]{:S(2)}, u32[]{:S(2)}) %collective-permute-start.1) | collective-permute-done | bytes 516128 | tf_op jit(solution)/shard_map/ppermute | solution.py:23
  60.4 4.7 %gather_fusion.5 = bf16[8,896,256]{2,1,0:T(8,128)(2,1)} fusion(bf16[8,896,256]{2,1,0:T(8,128)(2,1)} %bitcast.82, s32[1024]{0:T(1024)S(1)} %pad_clamp_fusion), kind=kCustom, calls=%fused_computation.2.clone | custom fusion | bytes 7340064 | tf_op jit(solution)/shard_map/jit(_take)/gather | solution.py:97
  65.0 4.6 %gather_fusion.4 = bf16[8,896,256]{2,1,0:T(8,128)(2,1)} fusion(bf16[8,896,256]{2,1,0:T(8,128)(2,1)} %bitcast.83, s32[1024]{0:T(1024)S(1)} %pad_clamp_fusion), kind=kCustom, calls=%fused_computation.clone | custom fusion | bytes 7340064 | tf_op jit(solution)/shard_map/jit(_take)/gather | solution.py:98
  69.6 5.9 %copy.42 = bf16[1,256,7168]{1,2,0:T(8,128)(2,1)} copy(bf16[1,256,7168]{2,1,0:T(8,128)(2,1)} %param.17) | data formatting | bytes 7340032 | tf_op args[6]
  75.5 6.2 %copy.43 = bf16[256,8,896]{2,0,1:T(8,128)(2,1)} copy(bf16[256,8,896]{0,2,1:T(8,128)(2,1)} %bitcast.77) | data formatting | bytes 7340032 | tf_op jit(solution)/shard_map/reshape;squeeze | solution.py:76
  81.7 4.8 %gather_fusion.2 = bf16[8,256,896]{2,1,0:T(8,128)(2,1)} fusion(bf16[256,8,896]{2,0,1:T(8,128)(2,1)} %copy.43, s32[1024]{0:T(1024)S(1)} %pad_clamp_fusion.1), kind=kCustom, calls=%fused_computation.6 | custom fusion | bytes 7340064 | tf_op jit(solution)/shard_map/jit(_take)/gather | solution.py:99
  91.5 19.3 %collective-permute-done.5 = bf16[4,144,896]{2,1,0:T(8,128)(2,1)S(1)} collective-permute-done((bf16[4,144,896]{2,1,0:T(8,128)(2,1)S(1)}, bf16[4,144,896]{2,1,0:T(8,128)(2,1)S(1)}, u32[]{:S(2)}, u32[]{:S(2)}) %collective-permute-start.5) | collective-permute-done | bytes 1032224 | tf_op jit(solution)/shard_map/ppermute | solution.py:23
  115.4 3.1 fusion.31
  118.5 3.1 fusion.26
  121.5 4.8 %gather_fusion.3 = bf16[8,256,896]{2,1,0:T(8,128)(2,1)} fusion(bf16[256,8,896]{2,0,1:T(8,128)(2,1)} %fusion.29, s32[1024]{0:T(1024)S(1)} %pad_clamp_fusion.1), kind=kCustom, calls=%fused_computation.7 | custom fusion | bytes 7340064 | tf_op jit(solution)/shard_map/jit(_take)/gather | solution.py:104
  126.4 6.3 %copy.44 = bf16[256,8,896]{0,2,1:T(8,128)(2,1)} copy(bf16[256,8,896]{2,0,1:T(8,128)(2,1)} %bitcast.81) | data formatting | bytes 7340032 | tf_op jit(solution)/shard_map/jit(_take)/gather | solution.py:104
  132.7 4.7 %gather_fusion.6 = bf16[8,896,256]{2,1,0:T(8,128)(2,1)} fusion(bf16[8,896,256]{2,1,0:T(8,128)(2,1)} %fusion.31, s32[1024]{0:T(1024)S(1)} %pad_clamp_fusion), kind=kCustom, calls=%fused_computation.1.clone | custom fusion | bytes 7340064 | tf_op jit(solution)/shard_map/jit(_take)/gather | solution.py:102
  137.3 4.7 %gather_fusion.7 = bf16[8,896,256]{2,1,0:T(8,128)(2,1)} fusion(bf16[8,896,256]{2,1,0:T(8,128)(2,1)} %fusion.26, s32[1024]{0:T(1024)S(1)} %pad_clamp_fusion), kind=kCustom, calls=%fused_computation.3.clone | custom fusion | bytes 7340064 | tf_op jit(solution)/shard_map/jit(_take)/gather | solution.py:103
  142.0 7.3 %fusion = bf16[256,7168]{0,1:T(8,128)(2,1)} fusion(bf16[256,8,896]{0,2,1:T(8,128)(2,1)} %copy.44, pred[7168]{0:T(1024)(128)(4,1)S(1)} %broadcast_in_dim.100), kind=kLoop, calls=%fused_computation.9 | loop fusion | flops 1835008 | bytes 7347200 | tf_op jit(solution)/shard_map/convert_element_type | solution.py:111
  149.3 5.1 %select_convert_fusion = (bf16[8,896,256]{2,1,0:T(8,128)(2,1)}, bf16[8,896,256]{2,1,0:T(8,128)(2,1)}) fusion(bf16[8,896,256]{2,1,0:T(8,128)(2,1)S(1)} %copy-done.3, pred[8]{0:T(512)(128)(4,1)S(1)} %compare_and_fusion.1, bf16[8,896,256]{2,1,0:T(8,128)(2,1)S(1)} %copy-done.2), kind=kLoop, calls=%fused_computation.10 | loop fusion | flops 3670016 | bytes 14680072 | tf_op jit(solution)/shard_map/convert_element_type | solution.py:110
  155.1 175.3 %all-reduce.3.cloned.1.call-done = (bf16[1,7168,256]{2,1,0:T(8,128)(2,1)}, bf16[1,256,7168]{1,2,0:T(8,128)(2,1)}) async-done(((bf16[1,7168,256]{2,1,0:T(8,128)(2,1)}, bf16[1,256,7168]{1,2,0:T(8,128)(2,1)}), (bf16[1,7168,256]{2,1,0:T(8,128)(2,1)}, bf16[1,256,7168]{1,2,0:T(8,128)(2,1)})) %all-reduce.3.cloned.1.call-update) | async-done | bytes 7340048 | tf_op jit(solution)/shard_map/psum | solution.py:110
  330.4 5.9 %copy.45 = bf16[1,256,7168]{2,1,0:T(8,128)(2,1)} copy(bf16[1,256,7168]{1,2,0:T(8,128)(2,1)} %get-tuple-element.18) | data formatting | bytes 7340032
  336.3 88.4 %all-gather.2.cloned.1.call-done = bf16[2,7168,256]{2,1,0:T(8,128)(2,1)} async-done(((bf16[1,7168,256]{2,1,0:T(8,128)(2,1)}), bf16[2,7168,256]{2,1,0:T(8,128)(2,1)}) %all-gather.2.cloned.1.call-update) | async-done | bytes 7340048 | tf_op jit(solution)/shard_map/all_gather | solution.py:12
  424.7 7.1 %reduce_sum.45 = bf16[7168,256]{1,0:T(8,128)(2,1)} reduce(bf16[2,7168,256]{2,1,0:T(8,128)(2,1)} %all-gather.2.cloned.1.call-done, bf16[]{:T(256)} %constant.89.clone.1), dimensions={0}, to_apply=%region_5.8 | reduce | flops 1835008 | bytes 11010050 | tf_op jit(solution)/shard_map/reduce_sum | solution.py:12
  431.9 4.2 copy.58
  (86 shorter events, 23.2 us)
Async XLA Ops:
  7.2 2.4 copy-start
  7.2 11.5 %copy-start.8 = (f32[128,8]{0,1:T(8,128)S(1)}, f32[128,8]{0,1:T(8,128)}, u32[]{:S(2)}) copy-start(f32[128,8]{0,1:T(8,128)} %param.14) | copy-start | bytes 12292
  10.3 8.7 %copy-start.4 = (bf16[128,7168]{1,0:T(8,128)(2,1)S(1)}, bf16[128,7168]{1,0:T(8,128)(2,1)}, u32[]{:S(2)}) copy-start(bf16[128,7168]{1,0:T(8,128)(2,1)} %param.12) | copy-start | bytes 5505028
  11.2 20.6 %all-to-all-start = ((bf16[16,9,896]{2,1,0:T(8,128)(2,1)}), bf16[16,9,896]{2,1,0:T(8,128)(2,1)S(1)}, u32[]{:S(2)}, u32[]{:S(2)}) async-start(bf16[16,9,896]{2,1,0:T(8,128)(2,1)} %bitcast.4), calls=%async_computation | async-start | bytes 917504 | tf_op jit(solution)/shard_map/all_to_all | solution.py:83
  32.0 5.2 %collective-permute-start = (bf16[1,144,896]{2,1,0:T(8,128)(2,1)S(1)}, bf16[1,144,896]{2,1,0:T(8,128)(2,1)S(1)}, u32[]{:S(2)}, u32[]{:S(2)}) collective-permute-start(bf16[1,144,896]{2,1,0:T(8,128)(2,1)S(1)} %reshape.147), channel_id=1, source_target_pairs={{0,2},{2,0},{4,6},{6,4},{8,10},{10,8},{12,14},{14,12},{16,18},{18,... | collective-permute-start | bytes 774152 | tf_op jit(solution)/shard_map/ppermute | solution.py:23
  33.1 17.3 %all-to-all-start.1 = ((bf16[16,9,896]{2,1,0:T(8,128)(2,1)}), bf16[16,9,896]{2,1,0:T(8,128)(2,1)S(1)}, u32[]{:S(2)}, u32[]{:S(2)}) async-start(bf16[16,9,896]{2,1,0:T(8,128)(2,1)} %bitcast.6), calls=%async_computation.1 | async-start | bytes 917504 | tf_op jit(solution)/shard_map/all_to_all | solution.py:84
  37.2 293.2 %all-reduce.3.cloned.1.call-start = ((), (), s32[]{:S(2)}) async-start(), calls=%async_computation.3 | async-start | bytes 14680064 | tf_op jit(solution)/shard_map/psum | solution.py:110
  37.3 18.9 %collective-permute-start.1 = (bf16[2,144,896]{2,1,0:T(8,128)(2,1)S(1)}, bf16[2,144,896]{2,1,0:T(8,128)(2,1)S(1)}, u32[]{:S(2)}, u32[]{:S(2)}) collective-permute-start(bf16[2,144,896]{2,1,0:T(8,128)(2,1)S(1)} %pad_maximum_fusion.2), channel_id=1, source_target_pairs={{0,4},{4,0},{2,6},{6,2},{8,12},{12,8},{10,14},{14,10},{16,20},{20,... | collective-permute-start | bytes 1548296 | tf_op jit(solution)/shard_map/ppermute | solution.py:23
  50.5 8.3 %collective-permute-start.3 = (bf16[1,144,896]{2,1,0:T(8,128)(2,1)S(1)}, bf16[1,144,896]{2,1,0:T(8,128)(2,1)S(1)}, u32[]{:S(2)}, u32[]{:S(2)}) collective-permute-start(bf16[1,144,896]{2,1,0:T(8,128)(2,1)S(1)} %reshape.149), channel_id=1, source_target_pairs={{0,2},{2,0},{4,6},{6,4},{8,10},{10,8},{12,14},{14,12},{16,18},{18,... | collective-permute-start | bytes 774152 | tf_op jit(solution)/shard_map/ppermute | solution.py:23
  57.3 30.2 %collective-permute-start.2 = (bf16[4,144,896]{2,1,0:T(8,128)(2,1)}, bf16[4,144,896]{2,1,0:T(8,128)(2,1)S(1)}, u32[]{:S(2)}, u32[]{:S(2)}) collective-permute-start(bf16[4,144,896]{2,1,0:T(8,128)(2,1)} %pad_maximum_fusion), channel_id=1, source_target_pairs={{0,8},{8,0},{2,10},{10,2},{4,12},{12,4},{6,14},{14,6},{16,24},{24,... | collective-permute-start | bytes 3096584 | tf_op jit(solution)/shard_map/ppermute | solution.py:23
  59.7 27.1 %collective-permute-start.4 = (bf16[2,144,896]{2,1,0:T(8,128)(2,1)}, bf16[2,144,896]{2,1,0:T(8,128)(2,1)S(1)}, u32[]{:S(2)}, u32[]{:S(2)}) collective-permute-start(bf16[2,144,896]{2,1,0:T(8,128)(2,1)} %pad_maximum_fusion.3), channel_id=1, source_target_pairs={{0,4},{4,0},{2,6},{6,2},{8,12},{12,8},{10,14},{14,10},{16,20},{20,... | collective-permute-start | bytes 1548296 | tf_op jit(solution)/shard_map/ppermute | solution.py:23
  86.6 2.0 copy-start.7
  86.9 23.9 %collective-permute-start.5 = (bf16[4,144,896]{2,1,0:T(8,128)(2,1)S(1)}, bf16[4,144,896]{2,1,0:T(8,128)(2,1)S(1)}, u32[]{:S(2)}, u32[]{:S(2)}) collective-permute-start(bf16[4,144,896]{2,1,0:T(8,128)(2,1)S(1)} %pad_maximum_fusion.1), channel_id=1, source_target_pairs={{0,8},{8,0},{2,10},{10,2},{4,12},{12,4},{6,14},{14,6},{16,24},{24,... | collective-permute-start | bytes 3096584 | tf_op jit(solution)/shard_map/ppermute | solution.py:23
  88.7 2.0 copy-start.6
  90.7 20.2 %copy-start.5 = (bf16[8,256,896]{2,1,0:T(8,128)(2,1)S(1)}, bf16[8,256,896]{2,1,0:T(8,128)(2,1)}, u32[]{:S(2)}) copy-start(bf16[8,256,896]{2,1,0:T(8,128)(2,1)} %gather_fusion.2) | copy-start | bytes 11010052
  142.0 7.3 %copy-start.2 = (bf16[8,896,256]{2,1,0:T(8,128)(2,1)S(1)}, bf16[8,896,256]{2,1,0:T(8,128)(2,1)}, u32[]{:S(2)}) copy-start(bf16[8,896,256]{2,1,0:T(8,128)(2,1)} %gather_fusion.6) | copy-start | bytes 11010052
  142.0 7.3 %copy-start.3 = (bf16[8,896,256]{2,1,0:T(8,128)(2,1)S(1)}, bf16[8,896,256]{2,1,0:T(8,128)(2,1)}, u32[]{:S(2)}) copy-start(bf16[8,896,256]{2,1,0:T(8,128)(2,1)} %gather_fusion.7) | copy-start | bytes 11010052
  154.4 270.4 %all-gather.2.cloned.1.call-start = ((), (), s32[]{:S(2)}) async-start(), calls=%async_computation.2 | async-start | bytes 11010048 | tf_op jit(solution)/shard_map/all_gather | solution.py:12
  431.9 4.2 copy-start.1
Sparse Core Ops, SparseCore 0:
  154.5 175.8 all-reduce.2
  332.5 92.1 all-gather.1
